TPU v7x, 32 devices: a whole 2x2x4 slice. The times are simulated.
32 devices in a mesh: intra: 4 (over y, x), inter: 8 (over z, core).
Axes of the slice: x: 2, y: 2, z: 4, core: 2. Of those that a mesh axis runs over, the one named last changes fastest.
Arguments:
- gate_pre: bfloat16 [1536, 14336], P('intra', 'inter'), may hold values from -6 to 6
- up_pre: bfloat16 [1536, 14336], P('intra', 'inter'), may hold values from -6 to 6
- cotangent: bfloat16 [1536, 8192], P('intra'), may hold values from -6 to 6
- weight_codes: bfloat16 [8192, 14336], P('intra', 'inter'), may hold values from -0.0625 to 0.0625
- weight_scale: bfloat16 [128, 14336], P('intra', 'inter'), may hold values from 0.5 to 2
- section_one: float32 [128, 14336], P(None, 'inter'), may hold values from 1 to 20
- section_two: float32 [128, 14336], P('intra', 'inter'), may hold values from 4 to 60
Outputs:
- grad_gate: bfloat16 [1536, 14336], P('intra', 'inter')
- grad_up: bfloat16 [1536, 14336], P('intra', 'inter')
- grad_codes: float32 [8192, 14336], P(('intra', 'inter'))
All inputs are finite; a program needn't handle non-finite values.
Results may differ from a plain program's by a relative error of at most 0.015.
Values may be sent and summed in bfloat16 or wider, within the bound.
A program may use at most 256 MiB of HBM per device.

v0:
```python
import functools

import jax
import jax.numpy as jnp
from jax import lax
from jax.experimental import pallas as pl
from jax.experimental.pallas import tpu as pltpu
from jax.sharding import PartitionSpec as P


def code_rows(blk, cols_ref, hidden_ref, one_ref, two_ref, out_ref):
    groups, tok, rows = cols_ref.shape
    total = [None] * (rows // blk)
    for a in range(groups):
        term = lax.dot_general(
            cols_ref[a], hidden_ref[a * tok:(a + 1) * tok, :], (((0,), (0,)), ((), ())),
            preferred_element_type=jnp.float32,
        )
        for b in range(rows // blk):
            coded = jnp.tanh(term[b * blk:(b + 1) * blk] * (1.0 / (7.0 * one_ref[b])))
            total[b] = coded if a == 0 else total[b] + coded
    for b in range(rows // blk):
        second = 7.0 * jnp.tanh(total[b] * (one_ref[b] / two_ref[b]))
        out_ref[b * blk:(b + 1) * blk, :] = second.astype(out_ref.dtype)


def recoded_rows(cols, hidden, one, two, blk):
    groups, tok, rows = cols.shape
    width = hidden.shape[1]
    tile = min(256, rows)
    scale_spec = pl.BlockSpec((tile // blk, 1, width), lambda i: (i, 0, 0))
    return pl.pallas_call(
        functools.partial(code_rows, blk),
        grid=(rows // tile,),
        in_specs=[
            pl.BlockSpec((groups, tok, tile), lambda i: (0, 0, i)),
            pl.BlockSpec((groups * tok, width), lambda i: (0, 0)),
            scale_spec,
            scale_spec,
        ],
        out_specs=pl.BlockSpec((tile, width), lambda i: (i, 0)),
        out_shape=jax.ShapeDtypeStruct((rows, width), jnp.bfloat16),
        cost_estimate=pl.CostEstimate(
            flops=2 * rows * width * groups * tok,
            bytes_accessed=2 * (cols.size + hidden.size + rows * width),
            transcendentals=(groups + 1) * rows * width,
        ),
        compiler_params=pltpu.CompilerParams(vmem_limit_bytes=40 * 2**20),
    )(cols, hidden, one, two)


def join_rows(*refs):
    start = 0
    for ref in refs[:-1]:
        refs[-1][:, start:start + ref.shape[1]] = ref[...].astype(jnp.float32)
        start += ref.shape[1]


def joined_rows(owned):
    sources, rows, _ = owned[0].shape
    width = sum(p.shape[2] for p in owned)
    return pl.pallas_call(
        join_rows,
        grid=(sources,),
        in_specs=[pl.BlockSpec((None, rows, p.shape[2]), lambda j: (j, 0, 0)) for p in owned],
        out_specs=pl.BlockSpec((rows, width), lambda j: (0, j)),
        out_shape=jax.ShapeDtypeStruct((rows, sources * width), jnp.float32),
        cost_estimate=pl.CostEstimate(
            flops=0, bytes_accessed=6 * sources * rows * width, transcendentals=0
        ),
        compiler_params=pltpu.CompilerParams(vmem_limit_bytes=24 * 2**20),
    )(*owned)


def on_device(gate_pre, up_pre, cotangent, weight_codes, weight_scale, section_one, section_two):
    width = weight_codes.shape[1]
    n_blocks = weight_scale.shape[0]
    blk = weight_codes.shape[0] // n_blocks
    n_intra = lax.axis_size("intra")
    n_inter = lax.axis_size("inter")
    own_rows = cotangent.shape[1] // n_intra
    tok = cotangent.shape[0]
    core = lax.axis_index("inter") % 2

    half = lax.dynamic_slice_in_dim(cotangent, core * (tok // 2), tok // 2, 0)
    mine = lax.all_to_all(
        half.reshape(tok // 2, n_intra, own_rows).transpose(1, 0, 2), "intra", 0, 0
    )
    other = lax.ppermute(mine, "inter", [(i, i ^ 1) for i in range(n_inter)])
    cols = jnp.concatenate(
        [jnp.where(core == 0, mine, other), jnp.where(core == 0, other, mine)], axis=1
    )

    gate_rows = gate_pre.astype(jnp.float32)
    up_rows = up_pre.astype(jnp.float32)
    sigma = jax.nn.sigmoid(gate_rows)
    gated = gate_rows * sigma
    hidden = (gated * up_rows).astype(jnp.bfloat16)
    one = lax.dynamic_slice_in_dim(
        section_one, lax.axis_index("intra") * n_blocks, n_blocks, 0
    ).reshape(n_blocks, 1, width)
    two = section_two.reshape(n_blocks, 1, width)

    cut = width // 128 * 3 // 7 * 128
    spans = [(0, cut), (cut, width)] if cut else [(0, width)]
    gathered = []
    piece = hidden
    for lo, hi in spans:
        piece = hidden[:, lo:hi]
        if gathered:
            piece, gathered[-1] = lax.optimization_barrier((piece, gathered[-1]))
        gathered.append(lax.all_gather(piece, "intra", axis=0, tiled=True))

    pieces = []
    for (lo, hi), full in zip(spans, gathered):
        pieces.append(recoded_rows(cols, full, one[:, :, lo:hi], two[:, :, lo:hi], blk))
        if len(pieces) == 1:
            pieces[0], late_cols = lax.optimization_barrier((pieces[0], cols))

    own_layer = (
        weight_codes.reshape(n_blocks, blk, width).astype(jnp.float32)
        * weight_scale.astype(jnp.float32)[:, None, :]
    ).astype(jnp.bfloat16).reshape(-1, width)
    partial_rows = jnp.dot(
        late_cols.reshape(n_intra * tok, own_rows), own_layer, preferred_element_type=jnp.float32
    ).astype(jnp.bfloat16)
    partial_rows, _ = lax.optimization_barrier((partial_rows, gathered[-1]))
    grad_hidden = lax.psum_scatter(
        partial_rows, "intra", scatter_dimension=0, tiled=True
    ).astype(jnp.float32)
    grad_gate = (grad_hidden * up_rows * sigma * (1.0 + gate_rows * (1.0 - sigma))).astype(
        jnp.bfloat16
    )
    grad_up = (grad_hidden * gated).astype(jnp.bfloat16)

    owned = [
        lax.all_to_all(
            p.reshape(n_inter, own_rows // n_inter, p.shape[1]), "inter", 0, 0
        )
        for p in pieces
    ]
    return (grad_gate, grad_up, joined_rows(owned))


def solution(mesh):
    placed = (
        P("intra", "inter"),
        P("intra", "inter"),
        P("intra", None),
        P("intra", "inter"),
        P("intra", "inter"),
        P(None, "inter"),
        P("intra", "inter"),
    )
    return jax.shard_map(
        on_device,
        mesh=mesh,
        in_specs=placed,
        out_specs=(P("intra", "inter"), P("intra", "inter"), P(("intra", "inter"), None)),
        check_vma=False,
    )
```

profile of v0, /device:TPU:25, one launch (start us, length us, event | category | flops | bytes accessed | tf_op | source)
XLA Modules:
  0.0 301.4 jit_solution(8174240332584194776)
XLA Ops:
  7.2 0.0 copy-start
  7.2 2.3 constant_dynamic-slice_fusion.1
  9.5 2.1 copy.13
  11.6 0.0 copy-start.10
  11.6 4.8 %all-to-all-start = ((bf16[4,192,2048]{2,1,0:T(8,128)(2,1)}), bf16[4,192,2048]{2,1,0:T(8,128)(2,1)}, u32[]{:S(2)}, u32[]{:S(2)}) async-start(bf16[4,192,2048]{2,1,0:T(8,128)(2,1)} %bitcast.19), calls=%async_computation | async-start | bytes 6291456 | tf_op jit(solution)/shard_map/all_to_all | solution.py:86
  16.3 0.0 all-gather.3.cloned.1.call-start
  16.4 0.0 copy-done.10
  16.4 2.2 fusion.1
  18.6 0.0 copy-start.12
  18.6 1.1 copy-done.12
  19.7 0.0 copy-start.14
  19.7 0.0 copy-start.15
  19.7 0.9 slice.25
  20.5 0.0 all-gather.3.cloned.1.call-update
  20.6 0.0 all-gather.5.cloned.1.call-start
  20.6 37.7 %all-to-all-done = bf16[4,192,2048]{2,1,0:T(8,128)(2,1)} async-done(((bf16[4,192,2048]{2,1,0:T(8,128)(2,1)}), bf16[4,192,2048]{2,1,0:T(8,128)(2,1)}, u32[]{:S(2)}, u32[]{:S(2)}) %all-to-all-start) | async-done | bytes 3145760 | tf_op jit(solution)/shard_map/all_to_all | solution.py:86
  58.3 1.4 collective-permute-start
  59.8 2.1 slice.24
  61.8 17.4 %all-gather.3.cloned.1.call-done.hidden_ref = bf16[1536,768]{1,0:T(8,128)(2,1)} async-done(((bf16[384,768]{1,0:T(8,128)(2,1)}), bf16[1536,768]{1,0:T(8,128)(2,1)}) %all-gather.3.cloned.1.call-update) | async-done | bytes 2359312 | tf_op jit(solution)/shard_map/all_gather | solution.py:112
  79.3 0.0 all-gather.5.cloned.1.call-update
  79.3 0.0 copy-done
  79.4 0.2 reshape.29
  79.6 0.0 copy-done.14
  79.6 0.2 reshape.30
  79.8 0.0 copy-start.13
  79.8 0.0 copy-done.15
  79.8 7.6 %fusion = bf16[2048,1792]{1,0:T(8,128)(2,1)} fusion(bf16[2048,1792]{1,0:T(8,128)(2,1)} %param.10, f32[32,1792]{1,0:T(8,128)S(1)} %convert_element_type.36), kind=kLoop, calls=%fused_computation.1 | loop fusion | flops 11010048 | bytes 14909440 | tf_op jit(solution)/shard_map/convert_element_type | solution.py:123
  87.4 0.0 copy-done.13
  87.4 0.0 collective-permute-done
  87.4 5.4 %broadcast_select_fusion.1 = (bf16[4,192,2048]{2,1,0:T(8,128)(2,1)S(1)}, bf16[4,192,2048]{2,1,0:T(8,128)(2,1)}) fusion(bf16[4,192,2048]{2,1,0:T(8,128)(2,1)} %all-to-all-done, bf16[4,192,2048]{2,1,0:T(8,128)(2,1)} %collective-permute-done, pred[]{:T(512)S(6)} %eq.6), kind=kLoop, calls=%fused_computation.12 | loop fusion | flops 3145728 | bytes 12582913 | tf_op jit(solution)/shard_map/jit(_where)/select_n | solution.py:91
  92.8 0.0 copy-start.9
  92.8 3.2 %pad_maximum_fusion.cols_ref = bf16[4,384,2048]{2,1,0:T(8,128)(2,1)S(1)} fusion(bf16[4,192,2048]{2,1,0:T(8,128)(2,1)} %get-tuple-element.14, bf16[4,192,2048]{2,1,0:T(8,128)(2,1)S(1)} %get-tuple-element.13), kind=kLoop, calls=%fused_computation.3 | loop fusion | flops 12582912 | bytes 12582912 | tf_op jit(solution)/shard_map/concatenate | solution.py:90
  96.0 0.0 copy-start.4
  96.0 2.6 copy-done.4
  98.7 0.0 copy-done.9
  98.7 9.7 %shard_map.94 = bf16[2048,768]{1,0:T(8,128)(2,1)S(1)} custom-call(bf16[4,384,2048]{2,1,0:T(8,128)(2,1)S(1)} %pad_maximum_fusion.cols_ref, bf16[1536,768]{1,0:T(8,128)(2,1)S(1)} %copy-done.9, f32[32,1,768]{2,1,0:T(1,128)S(1)} %slice.26.one_ref, f32[32,1,768]{2,1,0:T(1,128)S(1)} %slice.27.two_ref), custom_call_target="tpu_custom_call" | custom-call | flops 4831838208 | bytes 11796480 | tf_op jit(solution)/shard_map/pallas_call | solution.py:32
  108.4 0.0 copy-start.7
  108.4 1.6 copy-done.7
  110.0 5.7 %all-to-all-start.1 = ((bf16[8,256,768]{2,1,0:T(8,128)(2,1)}), bf16[8,256,768]{2,1,0:T(8,128)(2,1)S(1)}, u32[]{:S(2)}, u32[]{:S(2)}) async-start(bf16[8,256,768]{2,1,0:T(8,128)(2,1)} %bitcast.18), calls=%async_computation.2 | async-start | bytes 6291456 | tf_op jit(solution)/shard_map/all_to_all | solution.py:137
  115.7 0.0 reduce-scatter.2.cloned.1.call-start
  115.7 16.8 %convolution_convert_fusion = bf16[1536,1792]{1,0:T(8,128)(2,1)} fusion(bf16[1536,2048]{1,0:T(8,128)(2,1)} %bitcast.16, bf16[2048,1792]{1,0:T(8,128)(2,1)} %fusion), kind=kOutput, calls=%fused_computation.2 | convolution fusion | flops 11277041664 | bytes 19136512 | tf_op jit(solution)/shard_map/dot_general | solution.py:124
  132.6 0.0 all-gather.5.cloned.1.call-done.hidden_ref
  132.6 0.0 reduce-scatter.2.cloned.1.call-update
  132.6 0.9 slice.29.two_ref
  133.5 0.0 copy-start.5
  133.5 2.8 copy-done.5
  136.3 0.0 copy-start.8
  136.3 1.9 copy-done.8
  138.2 12.0 %shard_map.95 = bf16[2048,1024]{1,0:T(8,128)(2,1)S(1)} custom-call(bf16[4,384,2048]{2,1,0:T(8,128)(2,1)S(1)} %copy-done.5, bf16[1536,1024]{1,0:T(8,128)(2,1)S(1)} %copy-done.8, f32[32,1,1024]{2,1,0:T(1,128)S(1)} %slice.28.one_ref, f32[32,1,1024]{2,1,0:T(1,128)S(1)} %slice.29.two_ref), custom_call_target="tpu_custom_call" | custom-call | flops 6442450944 | bytes 13631488 | tf_op jit(solution)/shard_map/pallas_call | solution.py:32
  150.2 0.0 copy-start.6
  150.2 2.0 copy-done.6
  152.3 32.4 %all-to-all-done.1.refs_0_ = bf16[8,256,768]{2,1,0:T(8,128)(2,1)S(1)} async-done(((bf16[8,256,768]{2,1,0:T(8,128)(2,1)}), bf16[8,256,768]{2,1,0:T(8,128)(2,1)S(1)}, u32[]{:S(2)}, u32[]{:S(2)}) %all-to-all-start.1) | async-done | bytes 3145760 | tf_op jit(solution)/shard_map/all_to_all | solution.py:137
  184.6 0.0 copy-start.2
  184.6 1.6 copy-done.2
  186.3 0.0 copy-start.3
  186.3 97.8 %all_to_all.15.refs_1_ = bf16[8,256,1024]{2,1,0:T(8,128)(2,1)S(1)} all-to-all(bf16[8,256,1024]{2,1,0:T(8,128)(2,1)} %bitcast.17), channel_id=1, replica_groups=mesh['intra'=4,'inter'=8] {'inter'}, dimensions={0} | all-to-all | bytes 8388608 | tf_op jit(solution)/shard_map/all_to_all | solution.py:137
  284.1 0.0 copy-done.3
  284.1 0.0 copy-start.11
  284.1 0.0 copy-start.1
  284.1 6.1 %shard_map.96 = f32[256,14336]{1,0:T(8,128)} custom-call(bf16[8,256,768]{2,1,0:T(8,128)(2,1)S(1)} %copy-done.3, bf16[8,256,1024]{2,1,0:T(8,128)(2,1)S(1)} %all_to_all.15.refs_1_), custom_call_target="tpu_custom_call" | custom-call | bytes 22020096 | tf_op jit(solution)/shard_map/pallas_call | solution.py:62
  290.1 0.0 reduce-scatter.2.cloned.1.call-done
  290.1 0.0 copy-done.11
  290.1 4.7 %fusion.5 = (bf16[384,1792]{1,0:T(8,128)(2,1)}, bf16[384,1792]{1,0:T(8,128)(2,1)}) fusion(bf16[384,1792]{1,0:T(8,128)(2,1)} %reduce-scatter.2.cloned.1.call-done, bf16[384,1792]{1,0:T(8,128)(2,1)} %param.7, bf16[384,1792]{1,0:T(8,128)(2,1)S(1)} %copy-done.11), kind=kLoop, calls=%fused_computation.17 | loop fusion | flops 11010048 | bytes 6881280 | tf_op jit(solution)/shard_map/convert_element_type | solution.py:134
  294.9 0.0 copy-done.1
  (5 shorter events, 0.1 us)
Async XLA Ops:
  7.2 72.2 %copy-start = (f32[128,1792]{1,0:T(8,128)S(1)}, f32[128,1792]{1,0:T(8,128)}, u32[]{:S(2)}) copy-start(f32[128,1792]{1,0:T(8,128)} %param.12) | copy-start | bytes 2752516
  11.6 4.8 %copy-start.10 = (bf16[384,1792]{1,0:T(8,128)(2,1)S(1)}, bf16[384,1792]{1,0:T(8,128)(2,1)}, u32[]{:S(2)}) copy-start(bf16[384,1792]{1,0:T(8,128)(2,1)} %param.8) | copy-start | bytes 4128772
  11.6 46.8 %all-to-all-start = ((bf16[4,192,2048]{2,1,0:T(8,128)(2,1)}), bf16[4,192,2048]{2,1,0:T(8,128)(2,1)}, u32[]{:S(2)}, u32[]{:S(2)}) async-start(bf16[4,192,2048]{2,1,0:T(8,128)(2,1)} %bitcast.19), calls=%async_computation | async-start | bytes 6291456 | tf_op jit(solution)/shard_map/all_to_all | solution.py:86
  16.3 63.0 %all-gather.3.cloned.1.call-start = ((), (), s32[]{:S(2)}) async-start(), calls=%async_computation.4 | async-start | bytes 2949120 | tf_op jit(solution)/shard_map/all_gather | solution.py:112
  18.6 1.1 copy-start.12
  19.7 59.9 %copy-start.14 = (f32[32,1792]{1,0:T(8,128)S(1)}, f32[32,1792]{1,0:T(8,128)}, u32[]{:S(2)}) copy-start(f32[32,1792]{1,0:T(8,128)} %param.13) | copy-start | bytes 688132
  19.7 60.1 %copy-start.15 = (bf16[32,1792]{1,0:T(8,128)(2,1)S(1)}, bf16[32,1792]{1,0:T(8,128)(2,1)}, u32[]{:S(2)}) copy-start(bf16[32,1792]{1,0:T(8,128)(2,1)} %param.11) | copy-start | bytes 344068
  20.6 112.0 %all-gather.5.cloned.1.call-start = ((), (), s32[]{:S(2)}) async-start(), calls=%async_computation.5 | async-start | bytes 3932160 | tf_op jit(solution)/shard_map/all_gather | solution.py:112
  58.3 29.1 %collective-permute-start = (bf16[4,192,2048]{2,1,0:T(8,128)(2,1)}, bf16[4,192,2048]{2,1,0:T(8,128)(2,1)}, u32[]{:S(2)}, u32[]{:S(2)}) collective-permute-start(bf16[4,192,2048]{2,1,0:T(8,128)(2,1)} %all-to-all-done), channel_id=1, source_target_pairs={{0,1},{1,0},{2,3},{3,2},{4,5},{5,4},{6,7},{7,6},{8,9},{9,8},{10,11... | collective-permute-start | bytes 9437192 | tf_op jit(solution)/shard_map/ppermute | solution.py:89
  79.8 7.7 %copy-start.13 = (f32[32,1,1792]{2,1,0:T(1,128)}, f32[32,1,1792]{2,1,0:T(1,128)S(1)}, u32[]{:S(2)}) copy-start(f32[32,1,1792]{2,1,0:T(1,128)S(1)} %reshape.30) | copy-start | bytes 688132
  92.8 5.8 %copy-start.9 = (bf16[1536,768]{1,0:T(8,128)(2,1)S(1)}, bf16[1536,768]{1,0:T(8,128)(2,1)}, u32[]{:S(2)}) copy-start(bf16[1536,768]{1,0:T(8,128)(2,1)} %all-gather.3.cloned.1.call-done.hidden_ref) | copy-start | bytes 7077892
  96.0 2.6 copy-start.4
  108.4 1.6 copy-start.7
  110.0 74.6 %all-to-all-start.1 = ((bf16[8,256,768]{2,1,0:T(8,128)(2,1)}), bf16[8,256,768]{2,1,0:T(8,128)(2,1)S(1)}, u32[]{:S(2)}, u32[]{:S(2)}) async-start(bf16[8,256,768]{2,1,0:T(8,128)(2,1)} %bitcast.18), calls=%async_computation.2 | async-start | bytes 6291456 | tf_op jit(solution)/shard_map/all_to_all | solution.py:137
  115.7 174.4 %reduce-scatter.2.cloned.1.call-start = ((), (), s32[]{:S(2)}) async-start(), calls=%async_computation.6 | async-start | bytes 6881280 | tf_op jit(solution)/shard_map/reduce_scatter | solution.py:128
  133.5 2.8 copy-start.5
  136.3 1.9 copy-start.8
  150.2 2.0 copy-start.6
  184.6 1.6 copy-start.2
  186.3 97.8 %copy-start.3 = (bf16[8,256,768]{2,1,0:T(8,128)(2,1)S(1)}, bf16[8,256,768]{2,1,0:T(8,128)(2,1)}, u32[]{:S(2)}) copy-start(bf16[8,256,768]{2,1,0:T(8,128)(2,1)} %copy-done.2) | copy-start | bytes 9437188
  284.1 6.1 %copy-start.11 = (bf16[384,1792]{1,0:T(8,128)(2,1)S(1)}, bf16[384,1792]{1,0:T(8,128)(2,1)}, u32[]{:S(2)}) copy-start(bf16[384,1792]{1,0:T(8,128)(2,1)} %param.8) | copy-start | bytes 4128772
  284.1 10.8 %copy-start.1 = (f32[128,1792]{1,0:T(8,128)S(1)}, f32[128,1792]{1,0:T(8,128)}, u32[]{:S(2)}) copy-start(f32[128,1792]{1,0:T(8,128)} %param.12) | copy-start | bytes 2752516
Sparse Core Ops, SparseCore 0:
  20.7 58.5 all-gather.2
  81.7 43.8 all-gather.4
  132.7 63.0 reduce-scatter.1
where the time goes:
time: 306 us; the launch traced here: 301 us
  blocking collectives  97.8 us (32%)
  waiting for transfers between devices  87.6 us (29%)
  Pallas kernels  27.8 us (9%)
  other arithmetic  23.1 us (8%)
  local copies, waits for them, and re-layouts  22.3 us (7%)
  matrix products  16.8 us (5%)
  between operations  14 us (5%)
  starting transfers between devices  12 us (4%)
    all_to_all x1, blocking collectives, on_device(): lax.all_to_all(p.reshape(n_inter, own_rows // n_inter, p.shape[1]), 'inte...  97.8 us
    all_to_all x1, waiting for transfers between devices, on_device(): lax.all_to_all(half.reshape(tok // 2, n_intra, own_rows).transpose(1, 0,...  37.7 us
    all_to_all x1, waiting for transfers between devices, on_device(): lax.all_to_all(p.reshape(n_inter, own_rows // n_inter, p.shape[1]), 'inte...  32.4 us
    pallas_call x2, Pallas kernels, recoded_rows(): pl.pallas_call(functools.partial(code_rows, blk), grid=(rows // tile,), i...  21.8 us
    all_gather x2, waiting for transfers between devices, on_device(): gathered.append(lax.all_gather(piece, 'intra', axis=0, tiled=True))  17.5 us
    dot_general x1, matrix products, on_device(): jnp.dot(late_cols.reshape(n_intra * tok, own_rows), own_layer, preferred_...  16.8 us
    unnamed x32, local copies, waits for them, and re-layouts  13.7 us
    convert_element_type x1, other arithmetic, on_device(): own_layer = (weight_codes.reshape(n_blocks, blk, width).astype(jnp.float3...  7.61 us
  transfers between devices with their start and end apart: 6, of which 3 were waited for; matrix products, arithmetic and copies ran while one was open for 13% of the time, Pallas kernels for 9%

commit v1 on v0

v1 whole, which is shorter than its diff:
```python
import functools

import jax
import jax.numpy as jnp
from jax import lax
from jax.experimental import pallas as pl
from jax.experimental.pallas import tpu as pltpu
from jax.sharding import PartitionSpec as P

MESH = pl.DeviceIdType.MESH
LANES = 128
PIECE = 512


def times(n, x):
    return pl.multiple_of(x, n)


def bits_below(n):
    return [1 << k for k in range(n.bit_length() - 1)]


def xor(x, y, n):
    out = 0
    for bit in bits_below(n):
        one = lax.rem(lax.div(x, jnp.int32(bit)) + lax.div(jnp.int32(y), jnp.int32(bit)), jnp.int32(2))
        out = out + bit * one
    return out


def combos(masks):
    out = [0]
    for mask in masks:
        out = out + [c ^ mask for c in out]
    return out


def pieces(lo, hi, most=PIECE):
    out = []
    while lo < hi:
        out.append((lo, min(most, hi - lo)))
        lo += most
    return out


class Plan:
    def __init__(self, tok, model, width, rows, n_blocks, n_intra, n_inter):
        self.tok, self.model, self.width, self.rows = tok, model, width, rows
        self.blocks, self.blk = n_blocks, rows // n_blocks
        self.n_intra, self.n_inter = n_intra, n_inter
        self.own = rows // n_inter
        lanes = width // LANES
        self.swap = (lanes + 1) // 2 * LANES
        self.keep = width - self.swap
        self.wide = width + self.swap
        self.half = n_inter // 2
        self.near_rows = rows // 2
        self.quarter = rows // 4
        self.tile = max(self.own, LANES)
        self.share = [2, 1]
        self.n_share = 4
        self.dims = bits_below(n_intra)
        self.far_cols = pieces(0, self.keep)
        self.home_cols = pieces(self.keep, width)
        self.swap_cols = pieces(width, self.wide)
        self.hidden_cols = self.far_cols + self.home_cols + self.swap_cols
        self.sum_cols = pieces(0, width)

    def order(self, color):
        return self.dims[color:] + self.dims[:color]


def remote(src, dst, send, recv, device):
    return pltpu.make_async_remote_copy(
        src_ref=src, dst_ref=dst, send_sem=send, recv_sem=recv, device_id=device, device_id_type=MESH
    )


def main_kernel(
    plan,
    gate_hbm, up_hbm, cot_hbm, codes_hbm, scale_hbm, one_hbm, two_hbm,
    got_hbm, dgate_hbm, dup_hbm,
    gate, up, hid, cols, codes, scale, lay, inv, ratio, coded, part, sums,
    load_sem, xy_sem, share_sem, swap_sem, gather_sem, sum_sem, out_sem, own_sem, store_sem,
):
    p = plan
    i = lax.axis_index("intra")
    b = lax.axis_index("inter")
    n_a, n_b, tok = p.n_intra, p.n_inter, p.tok
    side = lax.div(b, jnp.int32(p.half))
    share_at = lax.rem(b, jnp.int32(p.n_share))
    part_tok = tok // p.n_share
    colors = len(p.dims)
    color_tok = tok // colors
    ia = functools.partial(xor, i, n=n_a)
    ib = functools.partial(xor, b, n=n_b)

    loads = [
        pltpu.make_async_copy(gate_hbm, gate, load_sem.at[0]),
        pltpu.make_async_copy(up_hbm, up, load_sem.at[1]),
        pltpu.make_async_copy(
            one_hbm.at[pl.ds(times(8, i * p.blocks), p.blocks)], inv.at[:, :p.width], load_sem.at[2]
        ),
        pltpu.make_async_copy(two_hbm, ratio.at[:, :p.width], load_sem.at[3]),
        pltpu.make_async_copy(
            cot_hbm.at[:, pl.ds(times(LANES, i * p.rows), p.rows)],
            cols.at[pl.ds(times(tok, i * tok), tok)],
            load_sem.at[4],
        ),
        pltpu.make_async_copy(codes_hbm, codes, load_sem.at[5]),
        pltpu.make_async_copy(scale_hbm, scale, load_sem.at[6]),
    ]
    for load in loads:
        load.start()

    barrier = pltpu.get_barrier_semaphore()
    for a in range(1, n_a):
        pl.semaphore_signal(barrier, inc=1, device_id=(ia(a), b), device_id_type=MESH)
    for a in range(1, n_b):
        pl.semaphore_signal(barrier, inc=1, device_id=(i, ib(a)), device_id_type=MESH)
    pl.semaphore_wait(barrier, n_a - 1 + n_b - 1)

    def row_start(step):
        toward = (1 - side) if step < 2 else side
        return times(LANES, toward * p.near_rows + (step % 2) * p.quarter)

    def across(step, a, sending):
        peer = ia(a)
        r0 = row_start(step)
        block = i if sending else peer
        src = cot_hbm.at[
            pl.ds(times(16, share_at * part_tok), part_tok),
            pl.ds(times(LANES, peer * p.rows + r0), p.quarter),
        ]
        dst = cols.at[
            pl.ds(times(16, block * tok + share_at * part_tok), part_tok), pl.ds(r0, p.quarter)
        ]
        k = step * (n_a - 1) + a - 1
        return remote(src, dst, xy_sem.at[0, k], xy_sem.at[1, k], (peer, b))

    def start_across(step):
        for a in range(1, n_a):
            across(step, a, True).start()

    def wait_across(step):
        for a in range(1, n_a):
            across(step, a, False).wait_recv()

    def shares(step, phase, sending):
        mask = p.share[phase]
        peer = ib(mask)
        r0 = row_start(step)
        out = []
        for a in range(1, n_a):
            for n, c in enumerate(combos(p.share[:phase])):
                at = xor(share_at, c if sending else c ^ mask, p.n_share)
                ref = cols.at[
                    pl.ds(times(16, ia(a) * tok + at * part_tok), part_tok), pl.ds(r0, p.quarter)
                ]
                k = (step * (n_a - 1) + a - 1) * (p.n_share - 1) + (1 << phase) - 1 + n
                out.append(remote(ref, ref, share_sem.at[0, k], share_sem.at[1, k], (i, peer)))
        return out

    def start_shares(step, phase):
        for copy in shares(step, phase, True):
            copy.start()

    def wait_shares(step, phase):
        for copy in shares(step, phase, False):
            copy.wait_recv()

    def gathers(piece, phase, sending):
        c0, w = p.hidden_cols[piece]
        out = []
        for color in range(colors):
            order = p.order(color)
            mask = order[phase]
            for n, c in enumerate(combos(order[:phase])):
                block = ia(c if sending else c ^ mask)
                ref = hid.at[
                    pl.ds(times(16, block * tok + color * color_tok), color_tok), c0:c0 + w
                ]
                k = (piece * colors + color) * (n_a - 1) + (1 << phase) - 1 + n
                out.append(remote(ref, ref, gather_sem.at[0, k], gather_sem.at[1, k], (ia(mask), b)))
        return out

    def start_gather(piece, phase):
        for copy in gathers(piece, phase, True):
            copy.start()

    def wait_gather(piece, phase):
        for copy in gathers(piece, phase, False):
            copy.wait_recv()

    def rest_of_gather(piece, phase):
        for q in range(phase, len(p.dims)):
            wait_gather(piece, q)
            if q + 1 < len(p.dims):
                start_gather(piece, q + 1)

    def make_hidden(piece):
        c0, w = p.hidden_cols[piece]
        step_tok = 64

        def body(t, carry):
            rows = pl.ds(times(step_tok, t * step_tok), step_tok)
            g = gate[rows, c0:c0 + w].astype(jnp.float32)
            u = up[rows, c0:c0 + w].astype(jnp.float32)
            h = g * jax.nn.sigmoid(g) * u
            hid[pl.ds(times(step_tok, i * tok + t * step_tok), step_tok), c0:c0 + w] = h.astype(hid.dtype)
            return carry

        lax.fori_loop(0, tok // step_tok, body, 0)

    n_half = p.blocks // 2

    def swaps(sending):
        other = ib(p.half)
        at = (1 - side) if sending else side
        rows = pl.ds(times(8, at * n_half), n_half)
        block = pl.ds(times(tok, i * tok), tok)
        out = []
        k = 0
        for buf, sel in ((hid, block), (inv, rows), (ratio, rows)):
            out.append(
                remote(
                    buf.at[sel, p.keep:p.width], buf.at[sel, p.width:p.wide],
                    swap_sem.at[0, k], swap_sem.at[1, k], (i, other),
                )
            )
            k += 1
        return out

    def prepare_scales():
        one = inv[:, :p.width]
        ratio[:, :p.width] = one / ratio[:, :p.width]
        inv[:, :p.width] = 1.0 / (7.0 * one)

    n_pieces = len(p.hidden_cols)
    per = p.tile // p.own

    def out_copy(owner, piece):
        c0, w = p.hidden_cols[piece]
        if c0 < p.width:
            source, at = b, c0
        else:
            source, at = ib(p.half), c0 - p.swap
        rel = ib(owner)
        k = rel * n_pieces + piece
        return remote(
            coded.at[pl.ds(times(16, owner * p.own), p.own), c0:c0 + w],
            got_hbm.at[source, :, at:at + w],
            out_sem.at[0, k], out_sem.at[1, k], (i, owner),
        )

    def own_copy(piece):
        c0, w = p.hidden_cols[piece]
        if c0 < p.width:
            source, at = b, c0
        else:
            source, at = ib(p.half), c0 - p.swap
        return pltpu.make_async_copy(
            coded.at[pl.ds(times(16, b * p.own), p.own), c0:c0 + w],
            got_hbm.at[source, :, at:at + w],
            own_sem.at[piece],
        )

    def make_coded(step, piece):
        c0, w = p.hidden_cols[piece]
        r0 = row_start(step)

        def body(t, carry):
            start = times(p.tile, r0 + t * p.tile)
            total = [None] * (p.tile // p.blk)
            for a in range(n_a):
                term = lax.dot_general(
                    cols[a * tok:(a + 1) * tok, pl.ds(start, p.tile)],
                    hid[a * tok:(a + 1) * tok, c0:c0 + w],
                    (((0,), (0,)), ((), ())),
                    preferred_element_type=jnp.float32,
                )
                for q in range(p.tile // p.blk):
                    at = lax.div(start, jnp.int32(p.blk)) + q
                    v = jnp.tanh(term[q * p.blk:(q + 1) * p.blk] * inv[pl.ds(at, 1), c0:c0 + w])
                    total[q] = v if a == 0 else total[q] + v
            for q in range(p.tile // p.blk):
                at = lax.div(start, jnp.int32(p.blk)) + q
                second = 7.0 * jnp.tanh(total[q] * ratio[pl.ds(at, 1), c0:c0 + w])
                coded[pl.ds(times(p.blk, start + q * p.blk), p.blk), c0:c0 + w] = second.astype(coded.dtype)
            for o in range(per):
                owner = lax.div(start, jnp.int32(p.own)) + o

                @pl.when(owner == b)
                def _():
                    own_copy(piece).start()

                @pl.when(owner != b)
                def _():
                    out_copy(owner, piece).start()
            return carry

        lax.fori_loop(0, p.quarter // p.tile, body, 0)

    sub = 256 if all(w % 256 == 0 for _, w in p.sum_cols) else LANES

    def make_partial(piece):
        c0, w = p.sum_cols[piece]

        def body(t, carry):
            at = times(LANES, c0 + t * sub)

            def scaled(n, inner):
                rows = pl.ds(times(p.blk, n * p.blk), p.blk)
                lay[rows, :] = (
                    codes[rows, pl.ds(at, sub)].astype(jnp.float32)
                    * scale[pl.ds(n, 1), pl.ds(at, sub)].astype(jnp.float32)
                ).astype(lay.dtype)
                return inner

            for n in range(p.blocks):
                scaled(n, 0)

            def block(a, inner):
                rows = pl.ds(times(tok, a * tok), tok)
                part[rows, pl.ds(at, sub)] = jnp.dot(
                    cols[rows, :], lay[...], preferred_element_type=jnp.float32
                ).astype(part.dtype)
                return inner

            lax.fori_loop(0, n_a, block, 0)
            return carry

        lax.fori_loop(0, w // sub, body, 0)

    def sum_copies(piece, phase, sending):
        c0, w = p.sum_cols[piece]
        out = []
        for color in range(colors):
            order = p.order(color)
            mask = order[phase]
            base = n_a - (n_a >> phase)
            for n, c in enumerate(combos(order[phase + 1:])):
                src = part.at[
                    pl.ds(times(16, ia(c ^ mask) * tok + color * color_tok), color_tok), c0:c0 + w
                ]
                dst = sums.at[
                    (base + n) * tok + color * color_tok:(base + n) * tok + (color + 1) * color_tok,
                    c0:c0 + w,
                ]
                k = (piece * colors + color) * (n_a - 1) + base + n
                out.append(
                    (remote(src, dst, sum_sem.at[0, k], sum_sem.at[1, k], (ia(mask), b)), color, base + n, c)
                )
        return out

    def start_sum(piece, phase):
        for copy, *_ in sum_copies(piece, phase, True):
            copy.start()

    def finish_sum(piece, phase):
        c0, w = p.sum_cols[piece]
        last = phase + 1 == len(p.dims)
        step_tok = 32
        for copy, color, slot, c in sum_copies(piece, phase, False):
            copy.wait_recv()

            def body(t, carry):
                mine = pl.ds(times(16, ia(c) * tok + color * color_tok + t * step_tok), step_tok)
                theirs = pl.ds(times(16, slot * tok + color * color_tok + t * step_tok), step_tok)
                both = part[mine, c0:c0 + w].astype(jnp.float32) + sums[theirs, c0:c0 + w].astype(jnp.float32)
                if not last:
                    part[mine, c0:c0 + w] = both.astype(part.dtype)
                else:
                    here = pl.ds(times(16, color * color_tok + t * step_tok), step_tok)
                    g = gate[here, c0:c0 + w].astype(jnp.float32)
                    u = up[here, c0:c0 + w].astype(jnp.float32)
                    sigma = jax.nn.sigmoid(g)
                    gate[here, c0:c0 + w] = (both * u * sigma * (1.0 + g * (1.0 - sigma))).astype(gate.dtype)
                    up[here, c0:c0 + w] = (both * (g * sigma)).astype(up.dtype)
                return carry

            lax.fori_loop(0, color_tok // step_tok, body, 0)
        if not last:
            start_sum(piece, phase + 1)
        else:
            for copy in stores(piece):
                copy.start()

    def stores(piece):
        c0, w = p.sum_cols[piece]
        return [
            pltpu.make_async_copy(src.at[:, c0:c0 + w], dst.at[:, c0:c0 + w], store_sem.at[2 * piece + n])
            for n, (src, dst) in enumerate(((gate, dgate_hbm), (up, dup_hbm)))
        ]

    far = list(range(len(p.far_cols)))
    home = [len(far) + n for n in range(len(p.home_cols))]
    swapped = [len(far) + len(home) + n for n in range(len(p.swap_cols))]
    n_sum = len(p.sum_cols)
    first, later = (far + home)[0], (far + home)[1:]
    later_far = [x for x in far if x != first]

    loads[0].wait()
    loads[1].wait()
    start_across(0)
    make_hidden(first)
    start_gather(first, 0)
    start_across(1)
    for x in home:
        make_hidden(x)
    for x in later_far:
        make_hidden(x)
    loads[2].wait()
    loads[3].wait()
    prepare_scales()
    loads[4].wait()
    wait_across(0)
    start_shares(0, 0)
    rest_of_gather(first, 0) if len(p.dims) == 1 else wait_gather(first, 0)
    if len(p.dims) > 1:
        start_gather(first, 1)
    start_across(2)
    start_across(3)
    wait_across(1)
    start_shares(1, 0)
    wait_shares(0, 0)
    start_shares(0, 1)
    for copy in swaps(True):
        copy.start()
    wait_shares(1, 0)
    start_shares(1, 1)
    for x in later:
        start_gather(x, 0)
    wait_across(2)
    start_shares(2, 0)
    rest_of_gather(first, 1)
    wait_shares(0, 1)
    make_coded(0, first)
    wait_across(3)
    start_shares(3, 0)
    wait_shares(2, 0)
    start_shares(2, 1)
    wait_shares(1, 1)
    make_coded(1, first)
    for x in later_far:
        wait_gather(x, 0)
        if len(p.dims) > 1:
            start_gather(x, 1)
    wait_shares(3, 0)
    start_shares(3, 1)
    wait_shares(2, 1)
    make_coded(2, first)
    wait_shares(3, 1)
    make_coded(3, first)
    for x in home:
        wait_gather(x, 0)
        if len(p.dims) > 1:
            start_gather(x, 1)
    for copy in swaps(False):
        copy.wait_recv()
    for x in swapped:
        start_gather(x, 0)
    for x in later_far:
        rest_of_gather(x, 1)
        for step in range(4):
            make_coded(step, x)
    loads[5].wait()
    loads[6].wait()
    make_partial(0)
    for x in swapped:
        wait_gather(x, 0)
        if len(p.dims) > 1:
            start_gather(x, 1)
    start_sum(0, 0)
    for x in home:
        rest_of_gather(x, 1)
        for step in (2, 3):
            make_coded(step, x)
    for n in range(1, n_sum):
        make_partial(n)
        start_sum(n, 0)
    for x in swapped:
        rest_of_gather(x, 1)
        for step in (2, 3):
            make_coded(step, x)
    for phase in range(len(p.dims)):
        for n in range(n_sum):
            finish_sum(n, phase)

    for n in range(n_sum):
        for copy in stores(n):
            copy.wait()
    for x in range(n_pieces):
        own_copy(x).wait()
        for rel in range(1, n_b if x in far else p.half):
            owner = ib(rel)
            copy = out_copy(owner, x)
            copy.wait_recv()
            copy.wait_send()
    for step in range(4):
        for a in range(1, n_a):
            across(step, a, True).wait_send()
        for phase in range(len(p.share)):
            for copy in shares(step, phase, True):
                copy.wait_send()
    for copy in swaps(True):
        copy.wait_send()
    for phase in range(len(p.dims)):
        for x in range(n_pieces):
            for copy in gathers(x, phase, True):
                copy.wait_send()
        for n in range(n_sum):
            for copy, *_ in sum_copies(n, phase, True):
                copy.wait_send()


def main_call(plan, gate, up, cot, codes, scale, one, two):
    p = plan
    bf16, f32 = jnp.bfloat16, jnp.float32
    vmem, dma = pltpu.VMEM, pltpu.SemaphoreType.DMA
    everywhere = pl.BlockSpec(memory_space=pl.ANY)
    gather = len(p.dims) * (p.n_intra - 1)
    flops = 4 * p.rows * p.width * p.n_intra * p.tok
    return pl.pallas_call(
        functools.partial(main_kernel, p),
        in_specs=[everywhere] * 7,
        out_specs=[everywhere] * 3,
        out_shape=[
            jax.ShapeDtypeStruct((p.n_inter, p.own, p.width), bf16),
            jax.ShapeDtypeStruct((p.tok, p.width), bf16),
            jax.ShapeDtypeStruct((p.tok, p.width), bf16),
        ],
        scratch_shapes=[
            vmem((p.tok, p.width), bf16),
            vmem((p.tok, p.width), bf16),
            vmem((p.n_intra * p.tok, p.wide), bf16),
            vmem((p.n_intra * p.tok, p.rows), bf16),
            vmem((p.rows, p.width), bf16),
            vmem((p.blocks, p.width), bf16),
            vmem((p.rows, 256 if all(w % 256 == 0 for _, w in p.sum_cols) else LANES), bf16),
            vmem((p.blocks, p.wide), f32),
            vmem((p.blocks, p.wide), f32),
            vmem((p.rows, p.wide), bf16),
            vmem((p.n_intra * p.tok, p.width), bf16),
            vmem(((p.n_intra - 1) * p.tok, p.width), bf16),
            dma((7,)),
            dma((2, 4 * (p.n_intra - 1))),
            dma((2, 4 * (p.n_intra - 1) * (p.n_share - 1))),
            dma((2, 3)),
            dma((2, len(p.hidden_cols) * gather)),
            dma((2, len(p.sum_cols) * gather)),
            dma((2, p.n_inter * len(p.hidden_cols))),
            dma((len(p.hidden_cols),)),
            dma((2 * len(p.sum_cols),)),
        ],
        cost_estimate=pl.CostEstimate(
            flops=flops, bytes_accessed=2 * flops // p.tok, transcendentals=5 * p.rows * p.width
        ),
        compiler_params=pltpu.CompilerParams(
            collective_id=0, has_side_effects=True, vmem_limit_bytes=63 * 2**20
        ),
    )(gate, up, cot, codes, scale, one, two)


def join_kernel(got, dgate, dup, codes_out, dgate_out, dup_out):
    codes_out[...] = got[...].astype(jnp.float32)
    dgate_out[...] = dgate[...]
    dup_out[...] = dup[...]


def join_call(got, dgate, dup):
    sources, rows, width = got.shape
    tok = dgate.shape[0]
    grads = pl.BlockSpec((tok // sources, width), lambda j: (j, 0))
    return pl.pallas_call(
        join_kernel,
        grid=(sources,),
        in_specs=[pl.BlockSpec((None, rows, width), lambda j: (j, 0, 0)), grads, grads],
        out_specs=[pl.BlockSpec((rows, width), lambda j: (0, j)), grads, grads],
        out_shape=[
            jax.ShapeDtypeStruct((rows, sources * width), jnp.float32),
            jax.ShapeDtypeStruct(dgate.shape, dgate.dtype),
            jax.ShapeDtypeStruct(dup.shape, dup.dtype),
        ],
        cost_estimate=pl.CostEstimate(
            flops=0, bytes_accessed=6 * got.size + 8 * dgate.size, transcendentals=0
        ),
        compiler_params=pltpu.CompilerParams(vmem_limit_bytes=24 * 2**20),
    )(got, dgate, dup)


def on_device(gate_pre, up_pre, cotangent, weight_codes, weight_scale, section_one, section_two):
    plan = Plan(
        cotangent.shape[0], cotangent.shape[1], weight_codes.shape[1], weight_codes.shape[0],
        weight_scale.shape[0], lax.axis_size("intra"), lax.axis_size("inter"),
    )
    got, dgate, dup = main_call(
        plan, gate_pre, up_pre, cotangent, weight_codes, weight_scale, section_one, section_two
    )
    codes_out, dgate, dup = join_call(got, dgate, dup)
    return dgate, dup, codes_out


def solution(mesh):
    placed = (
        P("intra", "inter"),
        P("intra", "inter"),
        P("intra", None),
        P("intra", "inter"),
        P("intra", "inter"),
        P(None, "inter"),
        P("intra", "inter"),
    )
    return jax.shard_map(
        on_device,
        mesh=mesh,
        in_specs=placed,
        out_specs=(P("intra", "inter"), P("intra", "inter"), P(("intra", "inter"), None)),
        check_vma=False,
    )
```

time: 306 us -> 183 us (0.60); the launches traced: 301 us -> 183 us
  Pallas kernels: 27.8 us -> 176 us
  blocking collectives: 97.8 us -> 0 us
  waiting for transfers between devices: 87.6 us -> 0 us
  other arithmetic: 23.1 us -> 0 us
  matrix products: 16.8 us -> 0 us
  local copies, waits for them, and re-layouts: 22.3 us -> 5.75 us
  between operations: 14 us -> 0.65 us
  starting transfers between devices: 12 us -> 0 us
    pallas_call x3 -> x2, Pallas kernels: 27.8 us -> 176 us  [the longest x1 170 us: main_call(): pl.pallas_call(functools.partial(main_kernel, p), in_specs=[everywhere] *...]
    all_to_all x1 -> x0, blocking collectives: 97.8 us -> none  [on_device(): lax.all_to_all(p.reshape(n_inter, own_rows // n_inter, p.shape[1]), 'inte...]
    all_to_all x2 -> x0, waiting for transfers between devices: 70.1 us -> none  [the longest x1 37.7 us: on_device(): lax.all_to_all(half.reshape(tok // 2, n_intra, own_rows).transpose(1, 0,...]
    all_gather x2 -> x0, waiting for transfers between devices: 17.5 us -> none  [on_device(): gathered.append(lax.all_gather(piece, 'intra', axis=0, tiled=True))]
    dot_general x1 -> x0, matrix products: 16.8 us -> none  [on_device(): jnp.dot(late_cols.reshape(n_intra * tok, own_rows), own_layer, preferred_...]
    convert_element_type x4 -> x0, other arithmetic: 14.6 us -> none  [the longest x1 7.61 us: on_device(): own_layer = (weight_codes.reshape(n_blocks, blk, width).astype(jnp.float3...]
    all_to_all x2 -> x0, starting transfers between devices: 10.5 us -> none  [the longest x1 5.67 us: on_device(): lax.all_to_all(p.reshape(n_inter, own_rows // n_inter, p.shape[1]), 'inte...]
    unnamed x32 -> x6, local copies, waits for them, and re-layouts: 13.7 us -> 5.75 us
  transfers between devices with their start and end apart: 6 -> 0, of which waited for: 3 -> 0; matrix products, arithmetic and copies ran while one was open for 13% -> 0% of each run, Pallas kernels for 9% -> 0%
where the time goes in v1:
time: 183 us
  Pallas kernels  176 us (96%)
  local copies, waits for them, and re-layouts  5.75 us (3%)
    pallas_call x1, Pallas kernels, main_call(): pl.pallas_call(functools.partial(main_kernel, p), in_specs=[everywhere] *...  170 us
    pallas_call x1, Pallas kernels, join_call(): pl.pallas_call(join_kernel, grid=(sources,), in_specs=[pl.BlockSpec((None...  6.53 us
    unnamed x6, local copies, waits for them, and re-layouts  5.75 us

profile of v1, /device:TPU:25, one launch (start us, length us, event | category | flops | bytes accessed | tf_op | source)
XLA Modules:
  0.0 182.9 jit_solution(12208924261853094852)
XLA Ops:
  0.6 169.9 %shard_map.94 = (bf16[8,256,1792]{2,1,0:T(8,128)(2,1)}, bf16[384,1792]{1,0:T(8,128)(2,1)}, bf16[384,1792]{1,0:T(8,128)(2,1)}) custom-call(bf16[384,1792]{1,0:T(8,128)(2,1)} %gate_hbm.1, bf16[384,1792]{1,0:T(8,128)(2,1)} %up_hbm.1, bf16[384,8192]{1,0:T(8,128)(2,1)} %cot_hbm.1, bf16[2048,1792]{1,0:T(8,128)(2,1)} %codes_hbm.1, bf16[32,1792]{1,0:T(8,128)(2,1)} %scale_hbm.1, ...), custom_call_target="tpu_custom_call" | custom-call | flops 22548578304 | bytes 117440512 | tf_op jit(solution)/shard_map/pallas_call | solution.py:524
  170.6 0.0 copy-start
  170.6 3.1 %copy-done = bf16[8,256,1792]{2,1,0:T(8,128)(2,1)S(1)} copy-done((bf16[8,256,1792]{2,1,0:T(8,128)(2,1)S(1)}, bf16[8,256,1792]{2,1,0:T(8,128)(2,1)}, u32[]{:S(2)}) %copy-start) | copy-done | bytes 7340056
  173.7 0.0 copy-start.1
  173.7 1.3 copy-done.1
  175.0 0.0 copy-start.2
  175.0 1.3 copy-done.2
  176.3 6.5 %shard_map.95 = (f32[256,14336]{1,0:T(8,128)}, bf16[384,1792]{1,0:T(8,128)(2,1)}, bf16[384,1792]{1,0:T(8,128)(2,1)}) custom-call(bf16[8,256,1792]{2,1,0:T(8,128)(2,1)S(1)} %copy-done, bf16[384,1792]{1,0:T(8,128)(2,1)S(1)} %copy-done.1, bf16[384,1792]{1,0:T(8,128)(2,1)S(1)} %copy-done.2), custom_call_target="tpu_custom_call" | custom-call | bytes 27525120 | tf_op jit(solution)/shard_map/pallas_call | solution.py:575
Async XLA Ops:
  170.6 3.1 %copy-start = (bf16[8,256,1792]{2,1,0:T(8,128)(2,1)S(1)}, bf16[8,256,1792]{2,1,0:T(8,128)(2,1)}, u32[]{:S(2)}) copy-start(bf16[8,256,1792]{2,1,0:T(8,128)(2,1)} %get-tuple-element.9.got) | copy-start | bytes 22020100
  173.7 1.3 copy-start.1
  175.0 1.3 copy-start.2

commit v2 on v1

--- a/solution.py
+++ b/solution.py
@@ -57,8 +57,8 @@
         self.near_rows = rows // 2
         self.quarter = rows // 4
         self.tile = max(self.own, LANES)
-        self.share = [2, 1]
-        self.n_share = 4
+        self.share = [[1], [1], [1], [1]]
+        self.most_shares = 2
         self.dims = bits_below(n_intra)
         self.far_cols = pieces(0, self.keep)
         self.home_cols = pieces(self.keep, width)
@@ -88,8 +88,10 @@
     b = lax.axis_index("inter")
     n_a, n_b, tok = p.n_intra, p.n_inter, p.tok
     side = lax.div(b, jnp.int32(p.half))
-    share_at = lax.rem(b, jnp.int32(p.n_share))
-    part_tok = tok // p.n_share
+    below = lax.rem(lax.div(b, jnp.int32(p.half // 2)), jnp.int32(2))
+    outer = 1 - lax.rem(side + below, jnp.int32(2))
+    early = outer * side + (1 - outer) * (1 - side)
+    late = 1 - early
     colors = len(p.dims)
     color_tok = tok // colors
     ia = functools.partial(xor, i, n=n_a)
@@ -120,13 +122,20 @@
         pl.semaphore_signal(barrier, inc=1, device_id=(i, ib(a)), device_id_type=MESH)
     pl.semaphore_wait(barrier, n_a - 1 + n_b - 1)
 
-    def row_start(step):
-        toward = (1 - side) if step < 2 else side
-        return times(LANES, toward * p.near_rows + (step % 2) * p.quarter)
+    def row_start(toward, q):
+        return times(LANES, toward * p.near_rows + q * p.quarter)
+
+    def step_rows(step):
+        return row_start(early if step < 2 else late, step % 2)
+
+    def share_of(step):
+        n = 1 << len(p.share[step])
+        return n, lax.rem(b, jnp.int32(n)), tok // n
 
     def across(step, a, sending):
         peer = ia(a)
-        r0 = row_start(step)
+        r0 = step_rows(step)
+        _, share_at, part_tok = share_of(step)
         block = i if sending else peer
         src = cot_hbm.at[
             pl.ds(times(16, share_at * part_tok), part_tok),
@@ -147,17 +156,18 @@
             across(step, a, False).wait_recv()
 
     def shares(step, phase, sending):
-        mask = p.share[phase]
+        mask = p.share[step][phase]
         peer = ib(mask)
-        r0 = row_start(step)
+        r0 = step_rows(step)
+        n_share, share_at, part_tok = share_of(step)
         out = []
         for a in range(1, n_a):
-            for n, c in enumerate(combos(p.share[:phase])):
-                at = xor(share_at, c if sending else c ^ mask, p.n_share)
+            for n, c in enumerate(combos(p.share[step][:phase])):
+                at = xor(share_at, c if sending else c ^ mask, n_share)
                 ref = cols.at[
                     pl.ds(times(16, ia(a) * tok + at * part_tok), part_tok), pl.ds(r0, p.quarter)
                 ]
-                k = (step * (n_a - 1) + a - 1) * (p.n_share - 1) + (1 << phase) - 1 + n
+                k = (step * (n_a - 1) + a - 1) * (p.most_shares - 1) + (1 << phase) - 1 + n
                 out.append(remote(ref, ref, share_sem.at[0, k], share_sem.at[1, k], (i, peer)))
         return out
 
@@ -265,9 +275,30 @@
             own_sem.at[piece],
         )
 
-    def make_coded(step, piece):
+    def send_tile(start, piece):
+        for o in range(per):
+            owner = lax.div(start, jnp.int32(p.own)) + o
+
+            @pl.when(owner == b)
+            def _():
+                own_copy(piece).start()
+
+            @pl.when(owner != b)
+            def _():
+                out_copy(owner, piece).start()
+
+    def send_coded(toward, q, piece):
+        r0 = row_start(toward, q)
+
+        def body(t, carry):
+            send_tile(times(p.tile, r0 + t * p.tile), piece)
+            return carry
+
+        lax.fori_loop(0, p.quarter // p.tile, body, 0)
+
+    def make_coded(toward, q, piece, now=None):
         c0, w = p.hidden_cols[piece]
-        r0 = row_start(step)
+        r0 = row_start(toward, q)
 
         def body(t, carry):
             start = times(p.tile, r0 + t * p.tile)
@@ -287,16 +318,10 @@
                 at = lax.div(start, jnp.int32(p.blk)) + q
                 second = 7.0 * jnp.tanh(total[q] * ratio[pl.ds(at, 1), c0:c0 + w])
                 coded[pl.ds(times(p.blk, start + q * p.blk), p.blk), c0:c0 + w] = second.astype(coded.dtype)
-            for o in range(per):
-                owner = lax.div(start, jnp.int32(p.own)) + o
-
-                @pl.when(owner == b)
-                def _():
-                    own_copy(piece).start()
-
-                @pl.when(owner != b)
-                def _():
-                    out_copy(owner, piece).start()
+            if now is None:
+                send_tile(start, piece)
+            else:
+                pl.when(now)(lambda: send_tile(start, piece))
             return carry
 
         lax.fori_loop(0, p.quarter // p.tile, body, 0)
@@ -397,92 +422,109 @@
     home = [len(far) + n for n in range(len(p.home_cols))]
     swapped = [len(far) + len(home) + n for n in range(len(p.swap_cols))]
     n_sum = len(p.sum_cols)
-    first, later = (far + home)[0], (far + home)[1:]
+    first = (far + home)[0]
     later_far = [x for x in far if x != first]
+    later_home = [x for x in home if x != first]
+
+    def next_gather(piece):
+        wait_gather(piece, 0)
+        if len(p.dims) > 1:
+            start_gather(piece, 1)
+
+    def finish_shares(step, phase=0):
+        for n in range(phase, len(p.share[step])):
+            wait_shares(step, n)
+            if n + 1 < len(p.share[step]):
+                start_shares(step, n + 1)
 
     loads[0].wait()
     loads[1].wait()
-    start_across(0)
     make_hidden(first)
     start_gather(first, 0)
-    start_across(1)
+    start_across(0)
     for x in home:
-        make_hidden(x)
-    for x in later_far:
-        make_hidden(x)
+        if x != first:
+            make_hidden(x)
     loads[2].wait()
     loads[3].wait()
     prepare_scales()
+
+    def start_swaps():
+        for copy in swaps(True):
+            copy.start()
+
+    start_swaps()
+    for x in later_far:
+        make_hidden(x)
+    next_gather(first)
+    for x in later_far:
+        start_gather(x, 0)
+    start_across(1)
     loads[4].wait()
     wait_across(0)
     start_shares(0, 0)
-    rest_of_gather(first, 0) if len(p.dims) == 1 else wait_gather(first, 0)
-    if len(p.dims) > 1:
-        start_gather(first, 1)
+    rest_of_gather(first, 1)
+    finish_shares(0)
+    if far:
+        make_coded(early, 0, first)
+    for x in later_far:
+        next_gather(x)
     start_across(2)
+    for x in later_home:
+        start_gather(x, 0)
     start_across(3)
     wait_across(1)
     start_shares(1, 0)
-    wait_shares(0, 0)
-    start_shares(0, 1)
-    for copy in swaps(True):
-        copy.start()
-    wait_shares(1, 0)
-    start_shares(1, 1)
-    for x in later:
-        start_gather(x, 0)
+    finish_shares(1)
+    if far:
+        make_coded(early, 1, first)
+    for x in later_far:
+        rest_of_gather(x, 1)
+        make_coded(early, 0, x)
+        make_coded(early, 1, x)
     wait_across(2)
     start_shares(2, 0)
-    rest_of_gather(first, 1)
-    wait_shares(0, 1)
-    make_coded(0, first)
+    for x in later_home:
+        next_gather(x)
     wait_across(3)
     start_shares(3, 0)
-    wait_shares(2, 0)
-    start_shares(2, 1)
-    wait_shares(1, 1)
-    make_coded(1, first)
-    for x in later_far:
-        wait_gather(x, 0)
-        if len(p.dims) > 1:
-            start_gather(x, 1)
-    wait_shares(3, 0)
-    start_shares(3, 1)
-    wait_shares(2, 1)
-    make_coded(2, first)
-    wait_shares(3, 1)
-    make_coded(3, first)
-    for x in home:
-        wait_gather(x, 0)
-        if len(p.dims) > 1:
-            start_gather(x, 1)
     for copy in swaps(False):
         copy.wait_recv()
     for x in swapped:
         start_gather(x, 0)
-    for x in later_far:
-        rest_of_gather(x, 1)
-        for step in range(4):
-            make_coded(step, x)
+    finish_shares(2)
+    finish_shares(3)
+    hold = outer * lax.rem(b, jnp.int32(2))
+    for x in far:
+        make_coded(late, 0, x, hold == 0)
+        make_coded(late, 1, x, hold == 0)
     loads[5].wait()
     loads[6].wait()
-    make_partial(0)
+    for n in range(n_sum // 2):
+        make_partial(n)
     for x in swapped:
-        wait_gather(x, 0)
-        if len(p.dims) > 1:
-            start_gather(x, 1)
-    start_sum(0, 0)
+        next_gather(x)
+    for n in range(n_sum // 2):
+        start_sum(n, 0)
     for x in home:
-        rest_of_gather(x, 1)
-        for step in (2, 3):
-            make_coded(step, x)
-    for n in range(1, n_sum):
+        if x != first:
+            rest_of_gather(x, 1)
+        make_coded(side, 0, x)
+        make_coded(side, 1, x)
+
+    @pl.when(hold == 1)
+    def _():
+        for x in far:
+            send_coded(late, 0, x)
+            send_coded(late, 1, x)
+
+    for n in range(n_sum // 2, n_sum):
         make_partial(n)
         start_sum(n, 0)
     for x in swapped:
         rest_of_gather(x, 1)
-        for step in (2, 3):
-            make_coded(step, x)
+        make_coded(side, 0, x)
+        make_coded(side, 1, x)
     for phase in range(len(p.dims)):
         for n in range(n_sum):
             finish_sum(n, phase)
@@ -500,7 +542,7 @@
     for step in range(4):
         for a in range(1, n_a):
             across(step, a, True).wait_send()
-        for phase in range(len(p.share)):
+        for phase in range(len(p.share[step])):
             for copy in shares(step, phase, True):
                 copy.wait_send()
     for copy in swaps(True):
@@ -545,7 +587,7 @@
             vmem(((p.n_intra - 1) * p.tok, p.width), bf16),
             dma((7,)),
             dma((2, 4 * (p.n_intra - 1))),
-            dma((2, 4 * (p.n_intra - 1) * (p.n_share - 1))),
+            dma((2, 4 * (p.n_intra - 1) * (p.most_shares - 1))),
             dma((2, 3)),
             dma((2, len(p.hidden_cols) * gather)),
             dma((2, len(p.sum_cols) * gather)),
@@ -585,7 +627,7 @@
         cost_estimate=pl.CostEstimate(
             flops=0, bytes_accessed=6 * got.size + 8 * dgate.size, transcendentals=0
         ),
-        compiler_params=pltpu.CompilerParams(vmem_limit_bytes=24 * 2**20),
+        compiler_params=pltpu.CompilerParams(vmem_limit_bytes=63 * 2**20),
     )(got, dgate, dup)
 
 

time: 183 us -> 172 us (0.940)
  local copies, waits for them, and re-layouts: 5.75 us -> 0 us
  Pallas kernels: 176 us -> 171 us
    pallas_call x1, Pallas kernels: 170 us -> 160 us  [main_call(): pl.pallas_call(functools.partial(main_kernel, p), in_specs=[everywhere] *...]
    unnamed x6 -> x0, local copies, waits for them, and re-layouts: 5.75 us -> none
    pallas_call x1, Pallas kernels: 6.53 us -> 11 us  [join_call(): pl.pallas_call(join_kernel, grid=(sources,), in_specs=[pl.BlockSpec((None...]
where the time goes in v2:
time: 172 us
  Pallas kernels  171 us (99%)
    pallas_call x1, Pallas kernels, main_call(): pl.pallas_call(functools.partial(main_kernel, p), in_specs=[everywhere] *...  160 us
    pallas_call x1, Pallas kernels, join_call(): pl.pallas_call(join_kernel, grid=(sources,), in_specs=[pl.BlockSpec((None...  11 us

profile of v2, /device:TPU:25, one launch (start us, length us, event | category | flops | bytes accessed | tf_op | source)
XLA Modules:
  0.0 171.6 jit_solution(13921061087732006367)
XLA Ops:
  0.6 160.0 %shard_map.94 = (bf16[8,256,1792]{2,1,0:T(8,128)(2,1)}, bf16[384,1792]{1,0:T(8,128)(2,1)}, bf16[384,1792]{1,0:T(8,128)(2,1)}) custom-call(bf16[384,1792]{1,0:T(8,128)(2,1)} %gate_hbm.1, bf16[384,1792]{1,0:T(8,128)(2,1)} %up_hbm.1, bf16[384,8192]{1,0:T(8,128)(2,1)} %cot_hbm.1, bf16[2048,1792]{1,0:T(8,128)(2,1)} %codes_hbm.1, bf16[32,1792]{1,0:T(8,128)(2,1)} %scale_hbm.1, ...), custom_call_target="tpu_custom_call" | custom-call | flops 22548578304 | bytes 117440512 | tf_op jit(solution)/shard_map/pallas_call | solution.py:566
  160.6 11.0 %shard_map.95 = (f32[256,14336]{1,0:T(8,128)}, bf16[384,1792]{1,0:T(8,128)(2,1)}, bf16[384,1792]{1,0:T(8,128)(2,1)}) custom-call(bf16[8,256,1792]{2,1,0:T(8,128)(2,1)} %get-tuple-element.9.got, bf16[384,1792]{1,0:T(8,128)(2,1)} %get-tuple-element.10.dgate, bf16[384,1792]{1,0:T(8,128)(2,1)} %get-tuple-element.11.dup), custom_call_target="tpu_custom_call" | custom-call | bytes 27525120 | tf_op jit(solution)/shard_map/pallas_call | solution.py:617
